TPU v7x, 32 devices: a whole 2x2x4 slice. The times are simulated.
32 devices in a mesh: grp: 4 (over y, x), row: 8 (over z, core).
Axes of the slice: x: 2, y: 2, z: 4, core: 2. Of those that a mesh axis runs over, the one named last changes fastest.
Arguments:
- serving: bfloat16 [16384, 128], P('row'), may hold values from -1 to 1
- serving_scale: bfloat16 [128], P('row'), may hold values from 0.099609375 to 1
- hot_blocks: int32 [4, 16], P('grp', 'row'), may hold values from 0 to 15, as said below
- bag_lengths: int32 [32, 256], P(('grp', 'row')), may hold values from 1 to 16, 1024 in all within a row
- bag_indices: int32 [32, 1024], P(('grp', 'row')), may hold values from 0 to 2047, as said below
- dense_act: bfloat16 [8192, 128], P(('grp', 'row')), may hold values from -6 to 6
- labels: float32 [8192], P(('grp', 'row')), may hold values from 0 to 1
- w_top: bfloat16 [256, 1024], replicated, may hold values from -0.375 to 0.375
- w_out: float32 [1024], replicated, may hold values from -0.012 to 0.012
- master: float32 [4, 4096, 128], P('grp', 'row'), may hold values from -0.3 to 0.3
- accum: float32 [4, 4096], P('grp', 'row'), may hold values from 1e-05 to 0.0001
Outputs:
- new_master: float32 [4, 4096, 128], P('grp', 'row')
- new_accum: float32 [4, 4096], P('grp', 'row')
- new_serving: bfloat16 [16384, 128], P('row')
- new_scale: bfloat16 [128], P('row')
- top_grad: float32 [256, 1024], replicated
Inputs may be any that keep to these rules, and one draw needn't show every extreme that they name: `hot_blocks`: the 2 entries that one group names in one row shard are distinct. `bag_indices`: in each device's line, exactly 64 distinct values lie in each range of 256 consecutive positions that starts at a multiple of 256.
All inputs are finite; a program needn't handle non-finite values. Where the computation divides by a largest or mean magnitude, that divisor is 1e-20 or more.
Results may differ from a plain program's by a relative error of at most 0.012.
Values may be sent and summed in bfloat16 or wider, within the bound.
A program may use at most 128 MiB of HBM per device.

v0:
```python
import math
import jax
import jax.numpy as jnp
from jax import lax
from jax.sharding import PartitionSpec as P

BLOCK = 128
MOST = 16
lr_step = 0.05


def pool_grad(table, lengths, indices, dense_d, labels_d, w_top, w_out):
    rows, width = table.shape
    total = indices.shape[0]
    ends = jnp.cumsum(lengths)
    starts = ends - lengths
    slots = jnp.arange(MOST, dtype=jnp.int32)
    positions = jnp.minimum(starts[:, None] + slots[None, :], total - 1)
    picked = jnp.where(slots[None, :] < lengths[:, None], indices[positions], -1)
    span = math.gcd(rows, 2048)
    pieces = rows // span

    def count_block(first):
        columns = first + jnp.arange(span, dtype=jnp.int32)
        return jnp.sum((picked[:, :, None] == columns[None, None, :]).astype(jnp.bfloat16), axis=1)

    counts = lax.map(count_block, jnp.arange(pieces, dtype=jnp.int32) * span)
    table_blocks = table.reshape(pieces, span, width)

    def add_block(running, pair):
        block_counts, block_rows = pair
        return (
            running
            + jnp.dot(
                block_counts.astype(jnp.float32), block_rows, precision=lax.Precision.HIGHEST
            ),
            None,
        )

    pooled, _ = lax.scan(
        add_block, jnp.zeros((lengths.shape[0], width), jnp.float32), (counts, table_blocks)
    )
    joined = jnp.concatenate([pooled.astype(jnp.bfloat16), dense_d], axis=1)
    pre = jnp.dot(joined, w_top, preferred_element_type=jnp.float32)
    sig = jax.nn.sigmoid(pre)
    logit = jnp.dot(pre * sig, w_out, precision=lax.Precision.HIGHEST)
    dlogit = jax.nn.sigmoid(logit) - labels_d
    dpre = (dlogit[:, None] * w_out[None, :] * (sig * (1.0 + pre * (1.0 - sig)))).astype(
        jnp.bfloat16
    )
    top = lax.dot_general(
        joined, dpre, (((0,), (0,)), ((), ())), preferred_element_type=jnp.float32
    )
    dz = lax.dot_general(dpre, w_top, (((1,), (1,)), ((), ())), preferred_element_type=jnp.float32)
    emb_grad = dz[:, :width]

    def spread_block(block_counts):
        weights = block_counts.astype(jnp.float32)
        summed = lax.dot_general(
            weights, emb_grad, (((0,), (0,)), ((), ())), precision=lax.Precision.HIGHEST
        )
        return (summed, jnp.sum(weights, axis=0))

    hot, column_use = lax.map(spread_block, counts)
    return (top, hot.reshape(rows, width), column_use.reshape(rows) > 0)


def on_device(
    serving,
    serving_scale,
    hot_blocks,
    bag_lengths,
    bag_indices,
    dense_act,
    labels,
    w_top,
    w_out,
    master,
    accum,
):
    width = serving.shape[1]
    chosen = hot_blocks[0]
    count = chosen.shape[0]
    local_blocks = serving.reshape(-1, BLOCK, width)
    total_blocks = local_blocks.shape[0]
    picked = local_blocks[chosen]
    picked_scale = serving_scale[chosen]
    fetched, fetched_scale = (
        lax.all_gather(picked, "row", axis=0, tiled=True),
        lax.all_gather(picked_scale, "row", axis=0, tiled=True),
    )
    table = (
        fetched.astype(jnp.float32) * fetched_scale.astype(jnp.float32)[:, None, None]
    ).reshape(-1, width)
    top_part, hot_part, used_rows = pool_grad(
        table, bag_lengths[0], bag_indices[0], dense_act, labels, w_top, w_out
    )
    top_grad = lax.psum(top_part, ("grp", "row"))
    owned = lax.psum_scatter(hot_part, "row", scatter_dimension=0, tiled=True).reshape(
        count, BLOCK, width
    )
    quarter = lax.axis_index("grp")
    groups = lax.axis_size("grp")
    per_owner = total_blocks // groups
    arrived, arrived_ids = (
        lax.all_gather(owned, "grp", axis=0, tiled=True),
        lax.all_gather(chosen.astype(jnp.float32), "grp", axis=0, tiled=True),
    )
    slot = arrived_ids.astype(jnp.int32) - quarter * per_owner
    inside = (slot >= 0) & (slot < per_owner)
    slot = jnp.where(inside, slot, per_owner)
    grad = (
        jnp.zeros((per_owner, BLOCK, width), jnp.float32)
        .at[slot]
        .add(arrived, mode="drop")
        .reshape(-1, width)
    )
    weights = master[0]
    state = accum[0]
    new_state = state + jnp.mean(grad * grad, axis=1)
    new_weights = weights - lr_step * grad / jnp.sqrt(new_state)[:, None]
    scale_new = (
        jnp.max(jnp.abs(new_weights.reshape(per_owner, BLOCK * width)), axis=1) + 1e-06
    ).astype(jnp.bfloat16)
    coded = (
        (
            new_weights.reshape(per_owner, BLOCK, width)
            / scale_new.astype(jnp.float32)[:, None, None]
        )
        .astype(jnp.bfloat16)
        .reshape(-1, width)
    )
    fresh, fresh_scale = (
        lax.all_gather(coded, "grp", axis=0, tiled=True),
        lax.all_gather(scale_new, "grp", axis=0, tiled=True),
    )
    return (new_weights[None], new_state[None], fresh, fresh_scale, top_grad)


def solution(mesh):
    return jax.shard_map(
        on_device,
        mesh=mesh,
        in_specs=(
            P("row", None),
            P("row"),
            P("grp", "row"),
            P(("grp", "row"), None),
            P(("grp", "row"), None),
            P(("grp", "row"), None),
            P(("grp", "row")),
            P(),
            P(),
            P("grp", "row", None),
            P("grp", "row"),
        ),
        out_specs=(P("grp", "row", None), P("grp", "row"), P("row", None), P("row"), P()),
        check_vma=False,
    )
```

profile of v0, /device:TPU:0, one launch (start us, length us, event | category | flops | bytes accessed | tf_op | source)
XLA Modules:
  0.0 261.1 jit_solution(4268729098067179809)
XLA Ops:
  8.0 0.0 reduce-scatter.2.cloned.1.call-start
  8.1 1.0 reduce-window.9
  9.1 0.1 slice.10
  9.2 0.1 slice_reduce_fusion
  9.3 0.8 bitcast_subtract_fusion
  10.1 0.1 compare_select_fusion
  10.2 0.1 reshape.249
  10.4 16.7 %gather_fusion = s32[4096]{0:T(1024)S(1)} fusion(s32[1024]{0:T(1024)S(1)} %bitcast.46, s32[4096]{0:T(1024)S(1)} %broadcast_clamp_fusion), kind=kCustom, calls=%fused_computation | custom fusion | bytes 49152 | tf_op jit(solution)/shard_map/gather | solution.py:19
  27.1 0.1 reshape.248
  27.2 0.1 fusion.8
  27.3 0.6 dynamic-slice.2
  28.6 0.6 gather_fusion.2
  29.2 0.2 dynamic-update-slice.1
  29.5 10.4 %fusion.1 = bf16[256,2048]{1,0:T(8,128)(2,1)S(1)} fusion(s32[256,16]{1,0:T(8,128)S(1)} %fusion.8), kind=kLoop, calls=%fused_computation.6 | loop fusion | flops 24641536 | bytes 1064960 | tf_op jit(solution)/shard_map/while/body/eval_jaxpr/reduce_sum | solution.py:25
  39.9 18.1 %all-reduce.1 = bf16[16]{0:T(256)(128)(2,1)S(1)} all-reduce(bf16[16]{0:T(256)(128)(2,1)S(1)} %dynamic-update-slice.1), channel_id=4, replica_groups=mesh['grp'=4,'row'=8] {'row'}, use_global_device_ids=true, to_apply=%add.1 | all-reduce | flops 16 | bytes 64
  58.0 0.6 gather_fusion.1
  58.6 15.1 %all-gather.1 = bf16[16,128,128]{2,1,0:T(8,128)(2,1)S(1)} all-gather(bf16[2,128,128]{2,1,0:T(8,128)(2,1)S(1)} %gather_fusion.1), channel_id=3, replica_groups=mesh['grp'=4,'row'=8] {'row'}, dimensions={0}, use_global_device_ids=true | all-gather | bytes 589824 | tf_op jit(solution)/shard_map/all_gather | solution.py:89
  73.7 0.1 copy.19
  73.8 0.1 convert_multiply_fusion
  74.0 1.0 convolution_convert_fusion
  75.0 0.0 copy-done.3
  75.0 0.3 fusion.10
  75.3 0.4 copy-done.9
  75.7 1.1 fusion.2
  76.8 0.4 multiply_convert_fusion
  77.2 0.3 fusion.5
  77.5 2.2 fusion.18
  79.7 0.0 all-reduce.5.cloned.1.call-start
  79.8 0.6 copy-done.12
  80.3 0.6 dynamic-slice.1
  81.6 0.1 bitcast_dynamic-update-slice_fusion
  81.7 9.9 %all-reduce = f32[8]{0:T(128)S(1)} all-reduce(f32[8]{0:T(128)S(1)} %bitcast_dynamic-update-slice_fusion), channel_id=2, replica_groups=mesh['grp'=4,'row'=8] {'grp'}, use_global_device_ids=true, to_apply=%add | all-reduce | flops 8 | bytes 64
  92.2 1.3 fusion.9
  93.5 17.2 %reduce-scatter.2.cloned.1.call-done = f32[256,128]{1,0:T(8,128)} async-done(((f32[2048,128]{1,0:T(8,128)}), f32[256,128]{1,0:T(8,128)}) %reduce-scatter.2.cloned.1.call-update) | async-done | bytes 131088 | tf_op jit(solution)/shard_map/reduce_scatter | solution.py:99
  110.8 10.3 %all_gather.21 = f32[8,128,128]{2,1,0:T(8,128)S(1)} all-gather(f32[2,128,128]{2,1,0:T(8,128)} %bitcast.51), channel_id=1, replica_groups=mesh['grp'=4,'row'=8] {'grp'}, dimensions={0}, use_global_device_ids=true | all-gather | bytes 655360 | tf_op jit(solution)/shard_map/all_gather | solution.py:106
  121.1 1.0 scatter_fusion
  122.2 0.1 broadcast_multiply_fusion
  122.4 0.8 abs_reduce_fusion
  123.2 0.1 bitcast_reduce_fusion
  123.3 0.2 dynamic-update-slice.2
  123.6 9.6 %all-reduce.2 = bf16[16]{0:T(256)(128)(2,1)} all-reduce(bf16[16]{0:T(256)(128)(2,1)S(1)} %dynamic-update-slice.2), channel_id=1, replica_groups=mesh['grp'=4,'row'=8] {'grp'}, use_global_device_ids=true, to_apply=%add.2 | all-reduce | flops 16 | bytes 64
  133.3 0.2 divide_convert_fusion
  133.4 9.7 %all_gather.22 = bf16[2048,128]{1,0:T(8,128)(2,1)S(1)} all-gather(bf16[512,128]{1,0:T(8,128)(2,1)S(1)} %bitcast.50), channel_id=1, replica_groups=mesh['grp'=4,'row'=8] {'grp'}, dimensions={0}, use_global_device_ids=true | all-gather | bytes 655360 | tf_op jit(solution)/shard_map/all_gather | solution.py:134
  143.1 0.6 add.103
  143.6 107.6 %all-reduce.5.cloned.1.call-done = f32[256,1024]{1,0:T(8,128)} async-done(((f32[256,1024]{1,0:T(8,128)}), f32[256,1024]{1,0:T(8,128)}) %all-reduce.5.cloned.1.call-update) | async-done | bytes 1048592 | tf_op jit(solution)/shard_map/psum | solution.py:98
  251.3 0.8 copy.26
  252.1 0.6 copy-done.5
  252.7 1.0 copy.27
  (40 shorter events, 0.2 us)
Async XLA Ops:
  8.0 50.0 %copy-start = (bf16[2048,128]{1,0:T(8,128)(2,1)S(1)}, bf16[2048,128]{1,0:T(8,128)(2,1)}, u32[]{:S(2)}) copy-start(bf16[2048,128]{1,0:T(8,128)(2,1)} %param.11) | copy-start | bytes 1572868
  8.0 2.3 copy-start.1
  8.0 102.7 %reduce-scatter.2.cloned.1.call-start = ((), (), s32[]{:S(2)}) async-start(), calls=%async_computation.1 | async-start | bytes 1179648 | tf_op jit(solution)/shard_map/reduce_scatter | solution.py:99
  10.3 16.8 %copy-start.8 = (s32[1,256]{1,0:T(1,128)S(1)}, s32[1,256]{1,0:T(1,128)}, u32[]{:S(2)}) copy-start(s32[1,256]{1,0:T(1,128)} %param.14) | copy-start | bytes 3076
  10.3 16.9 %copy-start.11 = (s32[1,2]{1,0:T(1,128)S(1)}, s32[1,2]{1,0:T(1,128)}, u32[]{:S(2)}) copy-start(s32[1,2]{1,0:T(1,128)} %param.13) | copy-start | bytes 28
  10.3 17.0 %copy-start.13 = (u32[32]{0:T(128)S(1)}, u32[32]{0:T(128)}, u32[]{:S(2)}) copy-start(u32[32]{0:T(128)} %constant.82) | copy-start | bytes 388
  10.4 18.2 %copy-start.2 = (bf16[16]{0:T(256)(128)(2,1)S(1)}, bf16[16]{0:T(256)(128)(2,1)}, u32[]{:S(2)}) copy-start(bf16[16]{0:T(256)(128)(2,1)} %param.12) | copy-start | bytes 100
  29.2 44.5 %copy-start.6 = (bf16[256,128]{1,0:T(8,128)(2,1)S(1)}, bf16[256,128]{1,0:T(8,128)(2,1)}, u32[]{:S(2)}) copy-start(bf16[256,128]{1,0:T(8,128)(2,1)} %param.16) | copy-start | bytes 196612
  73.9 1.0 copy-start.3
  75.0 0.7 copy-start.9
  75.7 1.1 copy-start.10
  79.7 0.7 copy-start.12
  79.7 171.5 %all-reduce.5.cloned.1.call-start = ((), (), s32[]{:S(2)}) async-start(), calls=%async_computation.2 | async-start | bytes 2097152 | tf_op jit(solution)/shard_map/psum | solution.py:98
  121.1 1.2 copy-start.7
  121.1 1.2 copy-start.4
  251.3 1.4 copy-start.5
Sparse Core Ops, SparseCore 0:
  79.8 30.8 reduce-scatter.1
Sparse Core Ops, SparseCore 1:
  123.7 127.5 all-reduce.4
where the time goes:
time: 262 us; the launch traced here: 261 us
  waiting for transfers between devices  125 us (48%)
  blocking collectives  72.7 us (28%)
  local copies, waits for them, and re-layouts  23.5 us (9%)
  between operations  17.8 us (7%)
  other arithmetic  16 us (6%)
  matrix products  6.17 us (2%)
    psum x1, waiting for transfers between devices, on_device(): top_grad = lax.psum(top_part, ('grp', 'row'))  108 us
    unnamed x3, blocking collectives  37.6 us
    reduce_scatter x1, waiting for transfers between devices, on_device(): lax.psum_scatter(hot_part, 'row', scatter_dimension=0, tiled=True)  17.2 us
    gather x2, local copies, waits for them, and re-layouts, pool_grad(): indices[positions]  16.8 us
    all_gather x1, blocking collectives, on_device(): lax.all_gather(picked, 'row', axis=0, tiled=True)  15.1 us
    reduce_sum x1, other arithmetic, count_block(): jnp.sum((picked[:, :, None] == columns[None, None, :]).astype(jnp.bfloat1...  10.4 us
    all_gather x1, blocking collectives, on_device(): lax.all_gather(owned, 'grp', axis=0, tiled=True)  10.3 us
    all_gather x1, blocking collectives, on_device(): lax.all_gather(coded, 'grp', axis=0, tiled=True)  9.65 us
  transfers between devices with their start and end apart: 2, of which 2 were waited for; matrix products, arithmetic and copies ran while one was open for 1% of the time, Pallas kernels for 0%

commit v1 on v0

--- a/solution.py
+++ b/solution.py
@@ -95,7 +95,9 @@
     top_part, hot_part, used_rows = pool_grad(
         table, bag_lengths[0], bag_indices[0], dense_act, labels, w_top, w_out
     )
-    top_grad = lax.psum(top_part, ("grp", "row"))
+    top_grad = top_part
+    for axis in ("row", "grp"):
+        top_grad = lax.psum(top_grad, axis)
     owned = lax.psum_scatter(hot_part, "row", scatter_dimension=0, tiled=True).reshape(
         count, BLOCK, width
     )

time: 262 us -> 235 us (0.90)
  waiting for transfers between devices: 125 us -> 97.6 us
  blocking collectives: 72.7 us -> 75.5 us
    psum x1 -> x2, waiting for transfers between devices: 108 us -> 63 us  [on_device(): top_grad = lax.psum(top_grad, axis)]
    reduce_scatter x1, waiting for transfers between devices: 17.2 us -> 34.6 us  [on_device(): lax.psum_scatter(hot_part, 'row', scatter_dimension=0, tiled=True)]
    all_gather x1, blocking collectives: 10.3 us -> 13.1 us  [on_device(): lax.all_gather(owned, 'grp', axis=0, tiled=True)]
  transfers between devices with their start and end apart: 2 -> 3, of which waited for: 2 -> 3; matrix products, arithmetic and copies ran while one was open for 1% -> 3% of each run, Pallas kernels for 0% -> 0%
where the time goes in v1:
time: 235 us
  waiting for transfers between devices  97.6 us (42%)
  blocking collectives  75.5 us (32%)
  local copies, waits for them, and re-layouts  23.5 us (10%)
  other arithmetic  16 us (7%)
  between operations  16 us (7%)
  matrix products  6.21 us (3%)
    psum x2, waiting for transfers between devices, on_device(): top_grad = lax.psum(top_grad, axis)  63 us
    unnamed x3, blocking collectives  37.5 us
    reduce_scatter x1, waiting for transfers between devices, on_device(): lax.psum_scatter(hot_part, 'row', scatter_dimension=0, tiled=True)  34.6 us
    gather x2, local copies, waits for them, and re-layouts, pool_grad(): indices[positions]  16.8 us
    all_gather x1, blocking collectives, on_device(): lax.all_gather(picked, 'row', axis=0, tiled=True)  15.1 us
    all_gather x1, blocking collectives, on_device(): lax.all_gather(owned, 'grp', axis=0, tiled=True)  13.1 us
    reduce_sum x1, other arithmetic, count_block(): jnp.sum((picked[:, :, None] == columns[None, None, :]).astype(jnp.bfloat1...  10.4 us
    all_gather x1, blocking collectives, on_device(): lax.all_gather(coded, 'grp', axis=0, tiled=True)  9.74 us
  transfers between devices with their start and end apart: 3, of which 3 were waited for; matrix products, arithmetic and copies ran while one was open for 3% of the time, Pallas kernels for 0%

profile of v1, /device:TPU:0, one launch (start us, length us, event | category | flops | bytes accessed | tf_op | source)
XLA Modules:
  0.0 234.9 jit_solution(3792107413024497601)
XLA Ops:
  7.2 1.0 reduce-window.9
  8.3 0.1 slice.10
  8.4 0.1 slice_reduce_fusion
  8.5 0.8 bitcast_subtract_fusion
  9.3 0.1 compare_select_fusion
  9.4 0.1 reshape.249
  9.5 16.7 %gather_fusion = s32[4096]{0:T(1024)S(1)} fusion(s32[1024]{0:T(1024)S(1)} %bitcast.46, s32[4096]{0:T(1024)S(1)} %broadcast_clamp_fusion), kind=kCustom, calls=%fused_computation | custom fusion | bytes 49152 | tf_op jit(solution)/shard_map/gather | solution.py:19
  26.2 0.1 reshape.248
  26.3 0.1 fusion.8
  26.5 0.6 dynamic-slice.2
  27.7 0.6 gather_fusion.2
  28.4 0.2 dynamic-update-slice.1
  28.6 10.4 %fusion.1 = bf16[256,2048]{1,0:T(8,128)(2,1)S(1)} fusion(s32[256,16]{1,0:T(8,128)S(1)} %fusion.8), kind=kLoop, calls=%fused_computation.6 | loop fusion | flops 24641536 | bytes 1064960 | tf_op jit(solution)/shard_map/while/body/eval_jaxpr/reduce_sum | solution.py:25
  39.0 18.1 %all-reduce.1 = bf16[16]{0:T(256)(128)(2,1)S(1)} all-reduce(bf16[16]{0:T(256)(128)(2,1)S(1)} %dynamic-update-slice.1), channel_id=4, replica_groups=mesh['grp'=4,'row'=8] {'row'}, use_global_device_ids=true, to_apply=%add.1 | all-reduce | flops 16 | bytes 64
  57.2 0.6 gather_fusion.1
  57.7 15.1 %all-gather.1 = bf16[16,128,128]{2,1,0:T(8,128)(2,1)S(1)} all-gather(bf16[2,128,128]{2,1,0:T(8,128)(2,1)S(1)} %gather_fusion.1), channel_id=3, replica_groups=mesh['grp'=4,'row'=8] {'row'}, dimensions={0}, use_global_device_ids=true | all-gather | bytes 589824 | tf_op jit(solution)/shard_map/all_gather | solution.py:89
  72.9 0.1 copy.19
  73.0 0.1 convert_multiply_fusion
  73.1 1.0 convolution_convert_fusion
  74.2 0.3 fusion.10
  74.5 0.4 copy-done.9
  74.8 1.1 fusion.2
  76.0 0.4 multiply_convert_fusion
  76.4 1.3 fusion.9
  77.7 0.0 reduce-scatter.2.cloned.1.call-start
  77.8 0.3 fusion.5
  78.1 2.2 fusion.18
  80.3 0.0 all-reduce.8.cloned.1.call-start
  80.3 0.6 copy-done.12
  80.9 0.6 dynamic-slice.1
  82.2 0.1 bitcast_dynamic-update-slice_fusion
  82.3 9.9 %all-reduce = f32[8]{0:T(128)S(1)} all-reduce(f32[8]{0:T(128)S(1)} %bitcast_dynamic-update-slice_fusion), channel_id=2, replica_groups=mesh['grp'=4,'row'=8] {'grp'}, use_global_device_ids=true, to_apply=%add | all-reduce | flops 8 | bytes 64
  92.8 42.7 %all-reduce.6.cloned.1.call-done = f32[256,1024]{1,0:T(8,128)} async-done(((f32[256,1024]{1,0:T(8,128)}), f32[256,1024]{1,0:T(8,128)}) %all-reduce.6.cloned.1.call-update) | async-done | bytes 1048592 | tf_op jit(solution)/shard_map/psum | solution.py:100
  135.5 34.6 %reduce-scatter.2.cloned.1.call-done = f32[256,128]{1,0:T(8,128)} async-done(((f32[2048,128]{1,0:T(8,128)}), f32[256,128]{1,0:T(8,128)}) %reduce-scatter.2.cloned.1.call-update) | async-done | bytes 131088 | tf_op jit(solution)/shard_map/reduce_scatter | solution.py:101
  170.1 13.1 %all_gather.21 = f32[8,128,128]{2,1,0:T(8,128)S(1)} all-gather(f32[2,128,128]{2,1,0:T(8,128)} %bitcast.51), channel_id=1, replica_groups=mesh['grp'=4,'row'=8] {'grp'}, dimensions={0}, use_global_device_ids=true | all-gather | bytes 655360 | tf_op jit(solution)/shard_map/all_gather | solution.py:108
  183.2 1.0 scatter_fusion
  184.3 0.1 broadcast_multiply_fusion
  184.5 0.8 abs_reduce_fusion
  185.3 0.1 bitcast_reduce_fusion
  185.4 0.2 dynamic-update-slice.2
  185.7 9.5 %all-reduce.2 = bf16[16]{0:T(256)(128)(2,1)} all-reduce(bf16[16]{0:T(256)(128)(2,1)S(1)} %dynamic-update-slice.2), channel_id=1, replica_groups=mesh['grp'=4,'row'=8] {'grp'}, use_global_device_ids=true, to_apply=%add.2 | all-reduce | flops 16 | bytes 64
  195.2 0.2 divide_convert_fusion
  195.4 9.7 %all_gather.22 = bf16[2048,128]{1,0:T(8,128)(2,1)S(1)} all-gather(bf16[512,128]{1,0:T(8,128)(2,1)S(1)} %bitcast.50), channel_id=1, replica_groups=mesh['grp'=4,'row'=8] {'grp'}, dimensions={0}, use_global_device_ids=true | all-gather | bytes 655360 | tf_op jit(solution)/shard_map/all_gather | solution.py:136
  205.1 0.6 add.105
  205.7 20.3 %all-reduce.8.cloned.1.call-done = f32[256,1024]{1,0:T(8,128)} async-done(((f32[256,1024]{1,0:T(8,128)}), f32[256,1024]{1,0:T(8,128)}) %all-reduce.8.cloned.1.call-update) | async-done | bytes 1048592 | tf_op jit(solution)/shard_map/psum | solution.py:100
  225.9 0.8 copy.27
  226.7 0.6 copy-done.5
  227.4 1.0 copy.28
  (43 shorter events, 0.3 us)
Async XLA Ops:
  7.2 50.0 %copy-start = (bf16[2048,128]{1,0:T(8,128)(2,1)S(1)}, bf16[2048,128]{1,0:T(8,128)(2,1)}, u32[]{:S(2)}) copy-start(bf16[2048,128]{1,0:T(8,128)(2,1)} %param.11) | copy-start | bytes 1572868
  7.2 2.3 copy-start.1
  7.2 128.3 %all-reduce.6.cloned.1.call-start = ((), (), s32[]{:S(2)}) async-start(), calls=%async_computation.2 | async-start | bytes 2097152 | tf_op jit(solution)/shard_map/psum | solution.py:100
  9.5 16.8 %copy-start.8 = (s32[1,256]{1,0:T(1,128)S(1)}, s32[1,256]{1,0:T(1,128)}, u32[]{:S(2)}) copy-start(s32[1,256]{1,0:T(1,128)} %param.14) | copy-start | bytes 3076
  9.5 16.9 %copy-start.11 = (s32[1,2]{1,0:T(1,128)S(1)}, s32[1,2]{1,0:T(1,128)}, u32[]{:S(2)}) copy-start(s32[1,2]{1,0:T(1,128)} %param.13) | copy-start | bytes 28
  9.5 17.0 %copy-start.13 = (u32[32]{0:T(128)S(1)}, u32[32]{0:T(128)}, u32[]{:S(2)}) copy-start(u32[32]{0:T(128)} %constant.82) | copy-start | bytes 388
  9.5 18.2 %copy-start.2 = (bf16[16]{0:T(256)(128)(2,1)S(1)}, bf16[16]{0:T(256)(128)(2,1)}, u32[]{:S(2)}) copy-start(bf16[16]{0:T(256)(128)(2,1)} %param.12) | copy-start | bytes 100
  28.4 44.5 %copy-start.6 = (bf16[256,128]{1,0:T(8,128)(2,1)S(1)}, bf16[256,128]{1,0:T(8,128)(2,1)}, u32[]{:S(2)}) copy-start(bf16[256,128]{1,0:T(8,128)(2,1)} %param.16) | copy-start | bytes 196612
  73.1 1.0 copy-start.3
  74.2 0.7 copy-start.9
  74.8 1.1 copy-start.10
  77.7 92.4 %reduce-scatter.2.cloned.1.call-start = ((), (), s32[]{:S(2)}) async-start(), calls=%async_computation.1 | async-start | bytes 1179648 | tf_op jit(solution)/shard_map/reduce_scatter | solution.py:101
  80.3 0.7 copy-start.12
  80.3 145.7 %all-reduce.8.cloned.1.call-start = ((), (), s32[]{:S(2)}) async-start(), calls=%async_computation.3 | async-start | bytes 2097152 | tf_op jit(solution)/shard_map/psum | solution.py:100
  183.2 1.2 copy-start.7
  183.2 1.2 copy-start.4
  225.9 1.4 copy-start.5
Sparse Core Ops, SparseCore 0:
  77.9 57.6 all-reduce.5
  138.4 31.6 reduce-scatter.1
  173.2 52.7 all-reduce.7
